TPU v7x, 128 devices: a whole 4x4x4 slice. The times are simulated.
128 devices in a mesh: seq: 64 (over x, z, y_hi, core), chan: 2 (over y_lo).
Axes of the slice: x: 4, y: 4 (y_hi: 2, y_lo: 2; y = y_hi * 2 + y_lo), z: 4, core: 2. Of those that a mesh axis runs over, the one named last changes fastest.
Arguments:
- signal: bfloat16 [524288, 256], P('seq', 'chan'), parts along dimension 1, may hold values from -6 to 6
- gate_values: bfloat16 [524288, 256], P('seq', 'chan'), parts along dimension 1, may hold values from -4 to 4
- skip_gain: float32 [256], P('chan'), parts along dimension 0, may hold values from 0.25 to 2
- filter_spectrum: bfloat16 [2, 512, 1024, 256], P(None, 'seq', None, 'chan'), parts along dimension 3, may hold values from -4 to 4, as said below
Outputs:
- gated_output: bfloat16 [524288, 256], P('seq', 'chan'), parts along dimension 1
There are 2 independent parts, one for each index of `chan`. A program takes and returns all parts, laid end to end along the dimension named above; each array names one. Nothing has to cross between parts.
Inputs may be any that keep to these rules, and one draw needn't show every extreme that they name: `filter_spectrum`: the spectrum of a real filter: the complex entry at frequency k equals the conjugate of the entry at frequency (524288 - k) mod 524288.
All inputs are finite; a program needn't handle non-finite values.
Results may differ from a plain program's by a relative error of at most 0.0085.
Values may be sent and summed in bfloat16 or wider, within the bound.
A program may use at most 128 MiB of HBM per device.

v0:
```python
import math

import jax
import jax.numpy as jnp
from jax import lax
from jax.sharding import PartitionSpec as P

OUTER = 1024
INNER = 512
SEQ = 524288


def tables(length):
    indices = lax.iota(jnp.int32, length)
    angles = (
        2.0 * math.pi / length * (indices[:, None] * indices[None, :] % length).astype(jnp.float32)
    )
    return (jnp.cos(angles).astype(jnp.bfloat16), jnp.sin(angles).astype(jnp.bfloat16))


def twiddle(c_values, b_values, length):
    angles = (
        2.0
        * math.pi
        / length
        * (c_values[:, None] * b_values[None, :] % length).astype(jnp.float32)
    )
    return (jnp.cos(angles), jnp.sin(angles))


def spectral_product(spectrum, filter_cols):
    spec_re = spectrum[0].astype(jnp.float32)
    spec_im = spectrum[1].astype(jnp.float32)
    filter_re = filter_cols[0].astype(jnp.float32)
    filter_im = filter_cols[1].astype(jnp.float32)
    return jnp.stack(
        [spec_re * filter_re - spec_im * filter_im, spec_re * filter_im + spec_im * filter_re]
    ).astype(jnp.bfloat16)


def local(signal, gate_values, skip_gain, filter_spectrum):
    shards = lax.axis_size("seq")
    own_index = lax.axis_index("seq")
    channels = signal.shape[1]
    outer_loc = OUTER // shards
    inner_loc = INNER // shards
    cos_a, sin_a = tables(OUTER)
    cos_b, sin_b = tables(INNER)
    inner_table = jnp.stack([cos_b, sin_b])
    outer_scale = 1.0 / math.sqrt(OUTER)
    inner_scale = 1.0 / math.sqrt(INNER)
    own_b = own_index * inner_loc + lax.iota(jnp.int32, inner_loc)
    own_c = own_index * outer_loc + lax.iota(jnp.int32, outer_loc)
    cols_cos, cols_sin = twiddle(lax.iota(jnp.int32, OUTER), own_b, SEQ)
    rows_cos, rows_sin = twiddle(own_c, lax.iota(jnp.int32, INNER), SEQ)
    cols_cos = cols_cos[:, :, None]
    cols_sin = cols_sin[:, :, None]
    rows_cos = rows_cos[:, :, None]
    rows_sin = rows_sin[:, :, None]
    signal_grid = signal.reshape(outer_loc, INNER, channels)
    pieces = lax.all_to_all(signal_grid, "seq", split_axis=1, concat_axis=0, tiled=True)
    breadth = pieces.shape[2]
    flattened = pieces.reshape(OUTER, inner_loc * breadth)
    fwd_re = jnp.dot(cos_a, flattened, preferred_element_type=jnp.float32).reshape(
        OUTER, inner_loc, breadth
    )
    fwd_im = -jnp.dot(sin_a, flattened, preferred_element_type=jnp.float32).reshape(
        OUTER, inner_loc, breadth
    )
    columns = jnp.stack(
        [
            (fwd_re * cols_cos + fwd_im * cols_sin) * outer_scale,
            (fwd_im * cols_cos - fwd_re * cols_sin) * outer_scale,
        ]
    ).astype(jnp.bfloat16)
    partials = jnp.einsum(
        "tdb,scbk->tscdk",
        inner_table,
        lax.all_to_all(columns, "seq", split_axis=1, concat_axis=2, tiled=True),
        preferred_element_type=jnp.float32,
    )
    spectrum = jnp.stack(
        [
            (partials[0, 0] + partials[1, 1]) * inner_scale,
            (partials[0, 1] - partials[1, 0]) * inner_scale,
        ]
    ).astype(jnp.bfloat16)
    filter_cols = lax.all_to_all(filter_spectrum, "seq", split_axis=2, concat_axis=1, tiled=True)
    product = spectral_product(spectrum, jnp.swapaxes(filter_cols, 1, 2))
    partials = jnp.einsum(
        "tbd,scdk->tscbk", inner_table, product, preferred_element_type=jnp.float32
    )
    back_re = (partials[0, 0] - partials[1, 1]) * inner_scale
    back_im = (partials[0, 1] + partials[1, 0]) * inner_scale
    rotated = jnp.stack(
        [back_re * rows_cos - back_im * rows_sin, back_re * rows_sin + back_im * rows_cos]
    ).astype(jnp.bfloat16)
    pieces = lax.all_to_all(rotated, "seq", split_axis=2, concat_axis=1, tiled=True)
    breadth = pieces.shape[3]
    convolved = (
        jnp.dot(
            cos_a, pieces[0].reshape(OUTER, inner_loc * breadth), preferred_element_type=jnp.float32
        )
        - jnp.dot(
            sin_a, pieces[1].reshape(OUTER, inner_loc * breadth), preferred_element_type=jnp.float32
        )
    ) * outer_scale
    by_columns = convolved.reshape(OUTER, inner_loc, breadth).astype(jnp.bfloat16)
    convolved = lax.all_to_all(by_columns, "seq", split_axis=0, concat_axis=1, tiled=True).reshape(
        outer_loc * INNER, channels
    )
    result = gate_values.astype(jnp.float32) * (
        convolved.astype(jnp.float32) + skip_gain[None, :] * signal.astype(jnp.float32)
    )
    return result.astype(jnp.bfloat16)


def solution(mesh):
    return jax.shard_map(
        local,
        mesh=mesh,
        in_specs=(P("seq", "chan"), P("seq", "chan"), P("chan"), P(None, "seq", None, "chan")),
        out_specs=P("seq", "chan"),
        check_vma=False,
    )
```

profile of v0, /device:TPU:9, one launch (start us, length us, event | category | flops | bytes accessed | tf_op | source)
XLA Modules:
  0.0 347.2 jit_solution(17635392218978430730)
XLA Ops:
  0.0 4.3 %copy.63 = bf16[16,512,128]{2,0,1:T(8,128)(2,1)} copy(bf16[16,512,128]{2,1,0:T(8,128)(2,1)} %bitcast.154) | data formatting | bytes 4194304 | tf_op jit(solution)/shard_map/reshape | solution.py:60
  4.3 10.7 %all-to-all-start = ((bf16[16,512,128]{2,0,1:T(8,128)(2,1)}), bf16[16,512,128]{2,0,1:T(8,128)(2,1)S(1)}, u32[]{:S(2)}, u32[]{:S(2)}) async-start(bf16[16,512,128]{2,0,1:T(8,128)(2,1)} %copy.63), calls=%async_computation | async-start | bytes 4194304 | tf_op jit(solution)/shard_map/all_to_all | solution.py:61
  15.0 6.9 %copy.73 = bf16[2,8,1024,128]{3,1,0,2:T(8,128)(2,1)} copy(bf16[2,8,1024,128]{3,2,1,0:T(8,128)(2,1)} %param.7) | data formatting | bytes 8388608 | tf_op args[3]
  21.9 24.2 %all-to-all-done = bf16[16,512,128]{2,0,1:T(8,128)(2,1)S(1)} async-done(((bf16[16,512,128]{2,0,1:T(8,128)(2,1)}), bf16[16,512,128]{2,0,1:T(8,128)(2,1)S(1)}, u32[]{:S(2)}, u32[]{:S(2)}) %all-to-all-start) | async-done | bytes 2097184 | tf_op jit(solution)/shard_map/all_to_all | solution.py:61
  46.1 5.4 %all-to-all-start.2 = ((bf16[2,8,1024,128]{3,1,0,2:T(8,128)(2,1)}), bf16[2,8,1024,128]{3,1,0,2:T(8,128)(2,1)}, u32[]{:S(2)}, u32[]{:S(2)}) async-start(bf16[2,8,1024,128]{3,1,0,2:T(8,128)(2,1)} %copy.73), calls=%async_computation.2 | async-start | bytes 8388608 | tf_op jit(solution)/shard_map/all_to_all | solution.py:88
  52.2 0.6 copy.118
  52.9 3.0 copy.66
  55.9 18.7 %fusion.34 = f32[1024,8,128]{2,0,1:T(8,128)S(1)} fusion(bf16[8,128,1024]{2,1,0:T(8,128)(2,1)} %bitcast.155), kind=kOutput, calls=%fused_computation.63 | convolution fusion | flops 2163212288 | bytes 6291456 | tf_op jit(solution)/shard_map/dot_general | solution.py:67
  74.6 19.1 %fusion.24 = (bf16[1,1024,8,128]{3,1,2,0:T(8,128)(2,1)S(1)}, bf16[1,1024,8,128]{3,1,2,0:T(8,128)(2,1)S(1)}) fusion(f32[1024,8,128]{2,0,1:T(8,128)S(1)} %fusion.34, f32[1024,8]{0,1:T(8,128)S(1)} %get-tuple-element.15, f32[1024,8]{0,1:T(8,128)S(1)} %get-tuple-element.14, bf16[8,128,1024]{2,1,0:T(8,128)(2,1)S(1)} %bitcast.156), kind=kOutput, calls=%fused_computation.52 | convolution fusion | flops 2174746624 | bytes 10551296 | tf_op jit(solution)/shard_map/dot_general | solution.py:64
  94.1 4.6 %copy.67 = bf16[2,1024,8,128]{3,2,0,1:T(8,128)(2,1)} copy(bf16[2,1024,8,128]{3,1,2,0:T(8,128)(2,1)S(1)} %pad_maximum_fusion) | data formatting | bytes 8388608 | tf_op jit(solution)/shard_map/stack | solution.py:70
  98.8 6.3 %all-to-all-done.2 = bf16[2,8,1024,128]{3,1,0,2:T(8,128)(2,1)} async-done(((bf16[2,8,1024,128]{3,1,0,2:T(8,128)(2,1)}), bf16[2,8,1024,128]{3,1,0,2:T(8,128)(2,1)}, u32[]{:S(2)}, u32[]{:S(2)}) %all-to-all-start.2) | async-done | bytes 4194336 | tf_op jit(solution)/shard_map/all_to_all | solution.py:88
  105.0 10.1 %all-to-all-start.1 = ((bf16[2,1024,8,128]{3,2,0,1:T(8,128)(2,1)}), bf16[2,1024,8,128]{3,2,0,1:T(8,128)(2,1)}, u32[]{:S(2)}, u32[]{:S(2)}) async-start(bf16[2,1024,8,128]{3,2,0,1:T(8,128)(2,1)} %copy.67), calls=%async_computation.1 | async-start | bytes 8388608 | tf_op jit(solution)/shard_map/all_to_all | solution.py:79
  115.2 4.3 %sine_convert_fusion.3 = (bf16[1,512,512]{2,1,0:T(8,128)(2,1)S(1)}, bf16[1,512,512]{2,1,0:T(8,128)(2,1)S(1)}) fusion(), kind=kLoop, calls=%fused_computation.74 | loop fusion | flops 4194304 | bytes 1048576 | tf_op jit(solution)/shard_map/convert_element_type | solution.py:18
  119.7 5.9 %copy.75 = bf16[2,64,8,16,128]{4,3,2,1,0:T(8,128)(2,1)} copy(bf16[2,64,8,16,128]{4,2,0,3,1:T(8,128)(2,1)} %bitcast.21) | data formatting | bytes 8388608 | tf_op jit(solution)/shard_map/all_to_all | solution.py:88
  125.6 7.6 %copy.76 = bf16[2,512,16,128]{1,3,2,0:T(8,128)(2,1)} copy(bf16[2,512,16,128]{3,2,1,0:T(8,128)(2,1)} %bitcast.149) | data formatting | bytes 8388608 | tf_op jit(solution)/shard_map/all_to_all | solution.py:88
  133.2 35.5 %all-to-all-done.1 = bf16[2,1024,8,128]{3,2,0,1:T(8,128)(2,1)} async-done(((bf16[2,1024,8,128]{3,2,0,1:T(8,128)(2,1)}), bf16[2,1024,8,128]{3,2,0,1:T(8,128)(2,1)}, u32[]{:S(2)}, u32[]{:S(2)}) %all-to-all-start.1) | async-done | bytes 4194336 | tf_op jit(solution)/shard_map/all_to_all | solution.py:79
  168.6 6.6 %convolution_bitcast_fusion.1 = f32[2,2,16,512,128]{3,4,0,2,1:T(8,128)S(1)} fusion(bf16[2,16,64,8,128]{4,3,0,1,2:T(8,128)(2,1)} %bitcast.12, bf16[1,512,512]{2,1,0:T(8,128)(2,1)S(1)} %get-tuple-element.18, bf16[1,512,512]{2,1,0:T(8,128)(2,1)S(1)} %get-tuple-element.19), kind=kOutput, calls=%fused_computation.1 | convolution fusion | flops 4297064448 | bytes 22020096 | tf_op jit(solution)/shard_map/tdb,scbk->tscdk/dot_general | solution.py:76
  175.2 3.2 fusion.1
  178.4 1.4 fusion.3
  179.8 4.7 %convolution_bitcast_fusion = f32[2,2,16,512,128]{3,4,0,2,1:T(8,128)S(1)} fusion(bf16[1,16,512,128]{2,3,1,0:T(8,128)(2,1)S(1)} %fusion.3, bf16[1,16,512,128]{2,3,1,0:T(8,128)(2,1)S(1)} %get-tuple-element.5, bf16[1,512,512]{2,1,0:T(8,128)(2,1)S(1)} %copy-done.5, bf16[1,512,512]{2,1,0:T(8,128)(2,1)S(1)} %copy-done.7), kind=kOutput, calls=%fused_computation | convolution fusion | flops 4305453056 | bytes 22020096 | tf_op jit(solution)/shard_map/tbd,scdk->tscbk/dot_general | solution.py:90
  184.5 2.7 subtract_convert_fusion
  187.2 2.3 pad_maximum_fusion.1
  189.5 7.9 %copy.80 = bf16[2,16,512,128]{3,1,0,2:T(8,128)(2,1)} copy(bf16[2,16,512,128]{2,3,1,0:T(8,128)(2,1)} %pad_maximum_fusion.1) | data formatting | bytes 8388608 | tf_op jit(solution)/shard_map/stack | solution.py:95
  197.4 63.8 %all_to_all.75 = bf16[2,16,512,128]{3,1,0,2:T(8,128)(2,1)S(1)} all-to-all(bf16[2,16,512,128]{3,1,0,2:T(8,128)(2,1)} %copy.80), channel_id=1, replica_groups=mesh['seq'=64,'chan'=2] {'seq'}, dimensions={2} | all-to-all | bytes 8388608 | tf_op jit(solution)/shard_map/all_to_all | solution.py:98
  261.2 1.6 copy.117
  263.9 17.1 %fusion.28 = f32[1024,1024]{0,1:T(8,128)S(1)} fusion(bf16[128,8,8,128]{3,2,1,0:T(8,128)(2,1)S(1)} %bitcast.159), kind=kOutput, calls=%fused_computation.56 | convolution fusion | flops 2163212288 | bytes 6291456 | tf_op jit(solution)/shard_map/dot_general | solution.py:104
  281.5 18.0 %multiply_convert_fusion = bf16[1024,1024]{0,1:T(8,128)(2,1)} fusion(f32[1024,1024]{0,1:T(8,128)S(1)} %fusion.28, bf16[128,8,8,128]{3,2,1,0:T(8,128)(2,1)S(1)} %bitcast.157), kind=kOutput, calls=%fused_computation.42 | convolution fusion | flops 2166358016 | bytes 8388608 | tf_op jit(solution)/shard_map/dot_general | solution.py:101
  299.5 3.4 copy.84
  302.9 39.0 %all_to_all.76 = bf16[1024,8,128]{2,1,0:T(8,128)(2,1)S(1)} all-to-all(bf16[1024,8,128]{2,1,0:T(8,128)(2,1)S(1)} %copy.84), channel_id=1, replica_groups=mesh['seq'=64,'chan'=2] {'seq'}, dimensions={0} | all-to-all | bytes 4194304 | tf_op jit(solution)/shard_map/all_to_all | solution.py:109
  342.9 1.1 copy-done.1
  344.0 0.6 copy-done.3
  344.7 2.1 fusion.19
  (27 shorter events, 4.0 us)
Async XLA Ops:
  4.3 41.8 %all-to-all-start = ((bf16[16,512,128]{2,0,1:T(8,128)(2,1)}), bf16[16,512,128]{2,0,1:T(8,128)(2,1)S(1)}, u32[]{:S(2)}, u32[]{:S(2)}) async-start(bf16[16,512,128]{2,0,1:T(8,128)(2,1)} %copy.63), calls=%async_computation | async-start | bytes 4194304 | tf_op jit(solution)/shard_map/all_to_all | solution.py:61
  46.1 58.9 %all-to-all-start.2 = ((bf16[2,8,1024,128]{3,1,0,2:T(8,128)(2,1)}), bf16[2,8,1024,128]{3,1,0,2:T(8,128)(2,1)}, u32[]{:S(2)}, u32[]{:S(2)}) async-start(bf16[2,8,1024,128]{3,1,0,2:T(8,128)(2,1)} %copy.73), calls=%async_computation.2 | async-start | bytes 8388608 | tf_op jit(solution)/shard_map/all_to_all | solution.py:88
  55.9 18.7 %copy-start.2 = (bf16[1024,1024]{1,0:T(8,128)(2,1)S(1)}, bf16[1024,1024]{1,0:T(8,128)(2,1)}, u32[]{:S(2)}) copy-start(bf16[1024,1024]{1,0:T(8,128)(2,1)} %copy.66) | copy-start | bytes 6291460
  105.0 63.6 %all-to-all-start.1 = ((bf16[2,1024,8,128]{3,2,0,1:T(8,128)(2,1)}), bf16[2,1024,8,128]{3,2,0,1:T(8,128)(2,1)}, u32[]{:S(2)}, u32[]{:S(2)}) async-start(bf16[2,1024,8,128]{3,2,0,1:T(8,128)(2,1)} %copy.67), calls=%async_computation.1 | async-start | bytes 8388608 | tf_op jit(solution)/shard_map/all_to_all | solution.py:79
  119.5 49.2 %copy-start.4 = (bf16[1,512,512]{2,1,0:T(8,128)(2,1)}, bf16[1,512,512]{2,1,0:T(8,128)(2,1)S(1)}, u32[]{:S(2)}) copy-start(bf16[1,512,512]{2,1,0:T(8,128)(2,1)S(1)} %get-tuple-element.18) | copy-start | bytes 1572868
  119.5 49.1 %copy-start.6 = (bf16[1,512,512]{2,1,0:T(8,128)(2,1)}, bf16[1,512,512]{2,1,0:T(8,128)(2,1)S(1)}, u32[]{:S(2)}) copy-start(bf16[1,512,512]{2,1,0:T(8,128)(2,1)S(1)} %get-tuple-element.19) | copy-start | bytes 1572868
  168.6 6.6 %copy-start = (bf16[2,512,16,128]{1,3,2,0:T(8,128)(2,1)S(1)}, bf16[2,512,16,128]{1,3,2,0:T(8,128)(2,1)}, u32[]{:S(2)}) copy-start(bf16[2,512,16,128]{1,3,2,0:T(8,128)(2,1)} %copy.76) | copy-start | bytes 12582916
  178.4 1.4 copy-start.5
  178.4 1.4 copy-start.7
  342.4 1.6 copy-start.1
  342.5 2.2 copy-start.3
  342.5 2.2 copy-start.8
where the time goes:
time: 354 us; the launch traced here: 347 us
  blocking collectives  103 us (29%)
  matrix products  84.1 us (24%)
  waiting for transfers between devices  65.9 us (19%)
  local copies, waits for them, and re-layouts  50.2 us (14%)
  starting transfers between devices  26.2 us (7%)
  other arithmetic  17.3 us (5%)
    all_to_all x1, blocking collectives, local(): lax.all_to_all(rotated, 'seq', split_axis=2, concat_axis=1, tiled=True)  63.8 us
    all_to_all x1, blocking collectives, local(): lax.all_to_all(by_columns, 'seq', split_axis=0, concat_axis=1, tiled=True)  39 us
    all_to_all x1, waiting for transfers between devices, local(): lax.all_to_all(columns, 'seq', split_axis=1, concat_axis=2, tiled=True)  35.5 us
    all_to_all x1, waiting for transfers between devices, local(): lax.all_to_all(signal_grid, 'seq', split_axis=1, concat_axis=0, tiled=True)  24.2 us
    dot_general x1, matrix products, local(): jnp.dot(cos_a, flattened, preferred_element_type=jnp.float32)  19.1 us
    dot_general x1, matrix products, local(): jnp.dot(sin_a, flattened, preferred_element_type=jnp.float32)  18.7 us
    dot_general x1, matrix products, local(): jnp.dot(cos_a, pieces[0].reshape(OUTER, inner_loc * breadth), preferred_e...  18 us
    dot_general x1, matrix products, local(): jnp.dot(sin_a, pieces[1].reshape(OUTER, inner_loc * breadth), preferred_e...  17.1 us
  transfers between devices with their start and end apart: 3, of which 3 were waited for; matrix products, arithmetic and copies ran while one was open for 21% of the time, Pallas kernels for 0%

commit v1 on v0

v1 whole, which is shorter than its diff:
```python
import math

import jax
import jax.numpy as jnp
import numpy as np
from jax import lax
from jax.experimental import pallas as pl
from jax.experimental.pallas import tpu as pltpu
from jax.sharding import PartitionSpec as P

MESH = pl.DeviceIdType.MESH
N = 64
H = N - 1
MULT = 27
OUTER = 1024
INNER = 512
SEQ = OUTER * INNER
BF = jnp.bfloat16
F32 = jnp.float32
SCALE = 1.0 / SEQ


def _circle(index, length):
    angle = 2.0 * np.pi / length * (index % length)
    return np.cos(angle), np.sin(angle)


def make_tables():
    a = np.arange(OUTER)
    c = np.arange(INNER)
    cos, sin = _circle(np.outer(c, a), OUTER)
    alt = 1.0 - 2.0 * (a % 2)
    fwd = np.stack([cos, -sin], 1)
    fwd[0, 1] = alt
    t1 = fwd.reshape(N, 8, 2, OUTER).transpose(0, 2, 1, 3).reshape(N, 16, OUTER)
    inv = 2.0 * fwd
    inv[0] = fwd[0]
    t4 = inv.reshape(N, 2, 4, 2, OUTER).transpose(1, 0, 2, 3, 4).reshape(1024, OUTER).T
    t4 = t4.reshape(N, 16, 1024)
    d = np.arange(INNER)
    cos, sin = _circle(np.outer(d, d), INNER)
    t2 = np.stack([np.stack([cos, sin], 0), np.stack([-sin, cos], 0)], 0)

    def blocks(m):
        m = m.reshape(2, 2, N, 8, N, 8).transpose(2, 0, 3, 4, 1, 5)
        return m.reshape(N, 16, 1024)

    d = np.arange(256)
    b = np.arange(INNER)
    cos0, sin0 = _circle(np.outer(d, b), INNER)
    cosh, sinh = _circle(np.outer(2 * d + 1, b), 2 * INNER)
    altb = 1.0 - 2.0 * (b % 2)
    s2 = np.zeros((2, 2, INNER, INNER))
    s2[0, 0, :256] = cos0
    s2[1, 0, :256] = -sin0
    s2[1, 0, 0] = altb
    s2[0, 1, 256:] = cosh
    s2[1, 1, 256:] = -sinh
    s3 = np.zeros((2, 2, INNER, INNER))
    s3[0, 0, :, :256] = 2 * cos0.T
    s3[0, 1, :, :256] = 2 * sin0.T
    s3[0, 0, :, 0] = 1.0
    s3[0, 1, :, 0] = -altb
    s3[1, 0, :, 256:] = -2 * cosh.T
    s3[1, 1, :, 256:] = -2 * sinh.T
    return t1, blocks(t2), blocks(s2), blocks(s3), t4


def peer(me, k):
    k = lax.rem(k * MULT, N)
    return (
        lax.rem(me // 16 + k // 16, 4) * 16
        + lax.rem(me // 4 + k // 4, 4) * 4
        + lax.rem(me // 2 + k // 2, 2) * 2
        + lax.rem(me + k, 2)
    )


def source(me, k):
    k = lax.rem(k * MULT, N)
    return (
        lax.rem(me // 16 + 4 - k // 16, 4) * 16
        + lax.rem(me // 4 + 16 - k // 4, 4) * 4
        + lax.rem(me // 2 + N - k // 2, 2) * 2
        + lax.rem(me + N - k, 2)
    )


def dot(x, y):
    return jnp.dot(x, y, preferred_element_type=F32)


def loop(n, body, start=0):
    def step(i, carry):
        body(i)
        return carry

    lax.fori_loop(start, n, step, 0)


def kernel(
    sig_h, filt_h, gate_h, skip, wt, t1_h, t2_h, t2s_h, t3s_h, t4_h, out_h,
    x1, fr, xf, x2, x4, x5, y2, y3, y4,
    t1, t2, t2s, t3s, t4, wb, fw, nyq, xb, tr, acc, prod, part, sig, gate, outv,
    ss, rs, ls,
):
    me = lax.axis_index("seq")
    ch = lax.axis_index("chan")
    bar = pltpu.get_barrier_semaphore()

    def hello(k):
        pl.semaphore_signal(bar, inc=1, device_id=(peer(me, k), ch), device_id_type=MESH)

    loop(N, hello, 1)
    pl.semaphore_wait(bar, H)

    def remote(src, dst, s, r, p):
        return pltpu.make_async_remote_copy(
            src, dst, ss.at[s], rs.at[r], device_id=(p, ch), device_id_type=MESH
        )

    def wait_recv(r, ref):
        remote(ref, ref, 0, r, me).wait_recv()

    def wait_send(s, ref):
        remote(ref, ref, s, 0, me).wait_send()

    def copy(src, dst, s):
        return pltpu.make_async_copy(src, dst, ls.at[s])

    def send1(k):
        p = peer(me, k)
        remote(sig_h.at[:, p], x1.at[me], 0, 0, p).start()

    loop(N, send1, 1)
    own1 = copy(sig_h.at[:, me], x1.at[me], 0)
    own1.start()

    def send_f(k):
        p = peer(me, k)
        remote(filt_h.at[:, :, p], fr.at[me], 1, 1, p).start()

    loop(N, send_f, 1)
    own_f = copy(filt_h.at[:, :, me], fr.at[me], 1)
    own_f.start()

    @pl.when(me == 0)
    def _():
        copy(filt_h.at[:, :, N], xf.at[0], 8).start()

    @pl.when((me > 0) & (me < 32))
    def _():
        remote(filt_h.at[:, :, N], xf.at[me], 2, 2, 0).start()

    special = 1 - jnp.minimum(me, 1)

    def load_tables(k):
        p = peer(me, k)
        copy(t1_h.at[p], t1.at[k], 2).start()
        copy(t2_h.at[p], t2.at[k], 3).start()
        copy(t2s_h.at[special, p], t2s.at[k], 4).start()
        copy(t3s_h.at[special, p], t3s.at[k], 5).start()
        copy(t4_h.at[p], t4.at[k], 6).start()

    loop(N, load_tables)
    sig_in = copy(sig_h, sig, 7)
    gate_in = copy(gate_h, gate, 9)
    sig_in.start()
    gate_in.start()

    def spread(u):
        w = wt[u]
        for j in range(16):
            wb[u, j] = jnp.broadcast_to(w[:, j : j + 1], (8, 128))

    loop(N, spread)

    def table_wait(ref, s):
        copy(ref, ref, s).wait()

    table_wait(t1, 2)
    table_wait(t2, 3)
    table_wait(t2s, 4)
    table_wait(t3s, 5)
    table_wait(t4, 6)

    wait_recv(0, x1.at[pl.ds(0, H)])
    own1.wait()

    def relay1(i):
        v = x1[pl.ds(i * 8, 8)].astype(F32).reshape(1024, 128)
        tr[...] = v
        for b in range(8):
            xb[pl.ds(pl.multiple_of(i * 128, 128), 128), b * 128 : (b + 1) * 128] = tr[
                pl.ds(b, 128, stride=8), :
            ].astype(BF)

    loop(8, relay1)

    def stage1(g):
        acc[...] = dot(t1[pl.ds(g * 16, 16)].reshape(256, 1024), xb[...])

        def twist(i):
            k = g * 16 + i
            u = peer(me, k)
            r0 = pl.multiple_of(i * 16, 16)
            base = 0
            for b in range(8):
                re = acc[pl.ds(r0, 8), b * 128 : (b + 1) * 128]
                im = acc[pl.ds(r0 + 8, 8), b * 128 : (b + 1) * 128]
                wc = wb[u, b]
                ws = wb[u, 8 + b]
                tr[pl.ds(base + b, 8, stride=16), :] = re * wc + im * ws
                tr[pl.ds(base + 8 + b, 8, stride=16), :] = im * wc - re * ws
            y2[k] = tr[0:128, :].reshape(8, 16, 128).astype(BF)

        loop(16, twist)

        def send2(i):
            k = g * 16 + i
            p = peer(me, k)

            @pl.when(k > 0)
            def _():
                remote(y2.at[k, pl.ds(0, 4)], x2.at[pl.ds(0, 4), me], 3, 3, p).start()

        loop(16, send2)

    loop(4, stage1)

    def send2b(k):
        p = peer(me, k)
        remote(y2.at[k, pl.ds(4, 4)], x2.at[pl.ds(4, 4), me], 4, 4, p).start()

    loop(N, send2b, 1)
    for j in range(8):
        x2[j, me] = y2[0, j]

    wait_recv(1, fr.at[pl.ds(0, H)])
    own_f.wait()

    def relay_f(v):
        tr[0:128, :] = fr[v].astype(F32).reshape(128, 128)
        for c in range(8):
            fw[c, v] = tr[pl.ds(c, 16, stride=8), :].astype(BF)

    loop(N, relay_f)

    @pl.when(me == 0)
    def _():
        copy(filt_h.at[:, :, N], xf.at[0], 8).wait()
        wait_recv(2, xf.at[pl.ds(0, 31)])
        nyq[...] = fw[0, 32].astype(F32)

        def relay_x(v):
            tr[0:128, :] = xf[v].astype(F32).reshape(128, 128)
            fw[0, 32 + v] = tr[pl.ds(0, 16, stride=8), :].astype(BF)

        loop(32, relay_x)

    for h in range(2):
        wait_recv(3 + h, x2.at[pl.ds(4 * h, 4), pl.ds(0, H)])
        cols = [x2[4 * h + j].reshape(1024, 128) for j in range(4)]
        for j in range(4):
            xb[:, j * 128 : (j + 1) * 128] = cols[j]

        def stage2(g):
            tab = t2[pl.ds(g * 16, 16)].reshape(256, 1024)
            if h == 0:
                tabs = t2s[pl.ds(g * 16, 16)].reshape(256, 1024)
                acc[:, 0:128] = dot(tabs, xb[:, 0:128])
                acc[:, 128:512] = dot(tab, xb[:, 128:512])
            else:
                acc[:, 0:512] = dot(tab, xb[:, 0:512])

            def multiply(i):
                v = peer(me, g * 16 + i)
                r0 = pl.multiple_of(i * 16, 16)
                for j in range(4):
                    sr = acc[pl.ds(r0, 8), j * 128 : (j + 1) * 128]
                    si = acc[pl.ds(r0 + 8, 8), j * 128 : (j + 1) * 128]
                    f = fw[4 * h + j, v].astype(F32)
                    fre = f[0:8]
                    fim = f[8:16]
                    pr = sr * fre - si * fim
                    pi = -(sr * fim + si * fre)
                    prod[pl.ds(pl.multiple_of(v * 16, 16), 16), j * 128 : (j + 1) * 128] = (
                        jnp.concatenate([pr, pi], axis=0).astype(BF)
                    )

            loop(16, multiply)
            if h == 0:

                @pl.when((me == 0) & (g == 0))
                def _():
                    sr = acc[0:8, 0:128]
                    si = acc[8:16, 0:128]
                    f = fw[0, 0].astype(F32)
                    fre = f[0:8]
                    fim = f[8:16]
                    rows = lax.broadcasted_iota(jnp.int32, (8, 128), 0)
                    pr = sr * fre - si * fim
                    pi = -(sr * fim + si * fre)
                    pr = jnp.where(rows == 0, sr * fre, pr)
                    pi = jnp.where(rows == 0, -(si * nyq[0:8]), pi)
                    prod[0:16, 0:128] = jnp.concatenate([pr, pi], axis=0).astype(BF)

        loop(4, stage2)

        def stage3(g):
            tab = t2[pl.ds(g * 16, 16)].reshape(256, 1024)
            if h == 0:
                tabs = t3s[pl.ds(g * 16, 16)].reshape(256, 1024)
                acc[:, 0:128] = dot(tabs, prod[:, 0:128])
                acc[:, 128:512] = dot(tab, prod[:, 128:512])
            else:
                acc[:, 0:512] = dot(tab, prod[...])

            def untwist(i):
                k = g * 16 + i
                t = peer(me, k)
                r0 = pl.multiple_of(i * 16, 16)
                for j in range(4):
                    re = acc[pl.ds(r0, 8), j * 128 : (j + 1) * 128]
                    im = acc[pl.ds(r0 + 8, 8), j * 128 : (j + 1) * 128]
                    wc = wb[t, 4 * h + j]
                    ws = wb[t, 8 + 4 * h + j]
                    y3[k, 4 * h + j] = jnp.concatenate(
                        [re * wc + im * ws, re * ws - im * wc], axis=0
                    ).astype(BF)

            loop(16, untwist)

            def send3(i):
                k = g * 16 + i
                p = peer(me, k)

                @pl.when(k > 0)
                def _():
                    remote(
                        y3.at[k, pl.ds(4 * h, 4)], x4.at[me, pl.ds(4 * h, 4)], 5 + h, 5 + h, p
                    ).start()

            loop(16, send3)

        loop(4, stage3)
        for j in range(4):
            x4[me, 4 * h + j] = y3[0, 4 * h + j]

    for h in range(2):
        wait_recv(5 + h, x4.at[pl.ds(0, H), pl.ds(4 * h, 4)])

        def relay4(i):
            v = x4[pl.ds(i * 2, 2), 4 * h : 4 * h + 4].astype(F32).reshape(128, 128)
            tr[0:128, :] = v
            for b in range(8):
                xb[pl.ds(pl.multiple_of(h * 512 + i * 16, 16), 16), b * 128 : (b + 1) * 128] = tr[
                    pl.ds(b, 16, stride=8), :
                ].astype(BF)

        loop(32, relay4)

        def stage4(g):
            rows = pl.ds(pl.multiple_of(g * 256, 256), 256)
            if h == 0:
                part[rows, :] = dot(
                    t4[pl.ds(g * 16, 16), :, 0:512].reshape(256, 512), xb[0:512, :]
                )
                return
            acc[...] = part[rows, :] + dot(
                t4[pl.ds(g * 16, 16), :, 512:1024].reshape(256, 512), xb[512:1024, :]
            )

            def finish(i):
                k = g * 16 + i
                r0 = pl.multiple_of(i * 16, 16)
                for b in range(8):
                    tr[pl.ds(b, 16, stride=8), :] = acc[pl.ds(r0, 16), b * 128 : (b + 1) * 128]
                y4[k] = (tr[0:128, :] * SCALE).reshape(16, 8, 128).astype(BF)

            loop(16, finish)

            def send4(i):
                k = g * 16 + i
                p = peer(me, k)

                @pl.when(k > 0)
                def _():
                    remote(y4.at[k], x5.at[me], 7, 7 + g, p).start()

            loop(16, send4)

        loop(4, stage4)

    x5[me] = y4[0]
    sig_in.wait()
    gate_in.wait()
    gain = skip[0:1, :].reshape(1, 1, 128)

    def last(g):
        if isinstance(g, int) and g == 0:
            wait_recv(7, x5.at[pl.ds(0, 15)])
        else:
            wait_recv(7 + g, x5.at[pl.ds(0, 16)])

        def gated(i):
            t = source(me, g * 16 + i)
            y = x5[t].astype(F32) + gain * sig[:, t].astype(F32)
            outv[:, t] = (gate[:, t].astype(F32) * y).astype(BF)

        loop(16, gated)

    for g in range(4):
        last(g)
    done = copy(outv, out_h, 10)
    done.start()
    wait_send(0, sig_h.at[:, pl.ds(0, H)])
    wait_send(1, filt_h.at[:, :, pl.ds(0, H)])

    @pl.when((me > 0) & (me < 32))
    def _():
        wait_send(2, filt_h.at[:, :, N])

    for h in range(2):
        wait_send(3 + h, y2.at[pl.ds(0, H), pl.ds(4 * h, 4)])
        wait_send(5 + h, y3.at[pl.ds(0, H), pl.ds(4 * h, 4)])
    wait_send(7, y4.at[pl.ds(0, H)])
    done.wait()


def local(signal, gate_values, skip_gain, filter_spectrum):
    me = lax.axis_index("seq")
    rows = lax.iota(jnp.int32, INNER)[:, None]
    lane = lax.iota(jnp.int32, 128)[None, :]
    own = me * 8 + lane % 8
    angle = 2.0 * math.pi / SEQ * (rows * own).astype(F32)
    wt = jnp.where(lane < 8, jnp.cos(angle), jnp.sin(angle)).reshape(N, 8, 128)
    t1, t2, s2, s3, t4 = make_tables()
    t2s = jnp.asarray(np.stack([t2, s2]), BF)
    t3s = jnp.asarray(np.stack([t2, s3]), BF)
    tabs = [jnp.asarray(t1, BF), jnp.asarray(t2, BF), t2s, t3s, jnp.asarray(t4, BF)]
    any_ = pl.BlockSpec(memory_space=pl.ANY)
    vm = pl.BlockSpec(memory_space=pltpu.VMEM)
    V = pltpu.VMEM
    dma = pltpu.SemaphoreType.DMA
    out = pl.pallas_call(
        kernel,
        out_shape=jax.ShapeDtypeStruct((16, 64, 8, 128), BF),
        in_specs=[any_, any_, any_, vm, vm] + [any_] * 5,
        out_specs=any_,
        scratch_shapes=[
            V((64, 16, 8, 128), BF),
            V((64, 2, 8, 8, 128), BF),
            V((32, 2, 8, 8, 128), BF),
            V((8, 64, 16, 128), BF),
            V((64, 8, 16, 128), BF),
            V((64, 16, 8, 128), BF),
            V((64, 8, 16, 128), BF),
            V((64, 8, 16, 128), BF),
            V((64, 16, 8, 128), BF),
            V((64, 16, 1024), BF),
            V((64, 16, 1024), BF),
            V((64, 16, 1024), BF),
            V((64, 16, 1024), BF),
            V((64, 16, 1024), BF),
            V((64, 16, 8, 128), F32),
            V((8, 64, 16, 128), BF),
            V((16, 128), F32),
            V((1024, 1024), BF),
            V((1024, 128), F32),
            V((256, 1024), F32),
            V((1024, 512), BF),
            V((1024, 1024), F32),
            V((16, 64, 8, 128), BF),
            V((16, 64, 8, 128), BF),
            V((16, 64, 8, 128), BF),
            dma((8,)),
            dma((12,)),
            dma((12,)),
        ],
        compiler_params=pltpu.CompilerParams(
            collective_id=0, has_side_effects=True, vmem_limit_bytes=67043328
        ),
    )(
        signal.reshape(16, 64, 8, 128),
        filter_spectrum.reshape(2, 8, 128, 8, 128),
        gate_values.reshape(16, 64, 8, 128),
        skip_gain.reshape(1, 128),
        wt,
        *tabs,
    )
    return out.reshape(8192, 128)


def solution(mesh):
    return jax.shard_map(
        local,
        mesh=mesh,
        in_specs=(P("seq", "chan"), P("seq", "chan"), P("chan"), P(None, "seq", None, "chan")),
        out_specs=P("seq", "chan"),
        check_vma=False,
    )
```

time: 354 us -> 158 us (0.45)
  the two profiles are of different devices: /device:TPU:9 before, /device:TPU:1 now
where the time goes in v1:
time: 158 us; the launch traced here: 155 us
  Pallas kernels  150 us (95%)
  local copies, waits for them, and re-layouts  3.05 us (2%)
  other arithmetic  1.8 us (1%)
    pallas_call x1, Pallas kernels, local(): pl.pallas_call(kernel, out_shape=jax.ShapeDtypeStruct((16, 64, 8, 128), B...  150 us

profile of v1, /device:TPU:1, one launch (start us, length us, event | category | flops | bytes accessed | tf_op | source)
XLA Modules:
  0.0 155.1 jit_solution(16414143336402299670)
XLA Ops:
  0.0 1.8 %sine_select_fusion.wt = f32[64,8,128]{2,1,0:T(8,128)} fusion(s32[128]{0:T(128)S(1)} %fusion, s32[64,8]{1,0:T(8,128)S(1)} %multiply_add_fusion, pred[128]{0:T(512)(128)(4,1)S(1)} %iota_compare_fusion), kind=kLoop, calls=%fused_computation | loop fusion | flops 262144 | bytes 264832 | tf_op jit(solution)/shard_map/jit(_where)/select_n | solution.py:437
  1.8 150.2 %shard_map.91 = bf16[16,64,8,128]{3,2,1,0:T(8,128)(2,1)} custom-call(bf16[16,64,8,128]{3,2,1,0:T(8,128)(2,1)} %bitcast.7, bf16[2,8,128,8,128]{4,3,2,1,0:T(8,128)(2,1)} %bitcast.6, bf16[16,64,8,128]{3,2,1,0:T(8,128)(2,1)} %bitcast.8, f32[1,128]{1,0:T(1,128)} %bitcast.9, f32[64,8,128]{2,1,0:T(8,128)} %sine_select_fusion.wt, ...), custom_call_target="tpu_custom_call" | custom-call | tf_op jit(solution)/shard_map/pallas_call | solution.py:446
  152.1 3.0 %copy.11 = bf16[8192,128]{1,0:T(8,128)(2,1)} copy(bf16[8192,128]{1,0:T(8,128)(2,1)} %bitcast.5) | data formatting | bytes 4194304
  (3 shorter events, 0.0 us)

commit v2 on v1

v2 whole, which is shorter than its diff:
```python
import math

import jax
import jax.numpy as jnp
import numpy as np
from jax import lax
from jax.experimental import pallas as pl
from jax.experimental.pallas import tpu as pltpu
from jax.sharding import PartitionSpec as P

MESH = pl.DeviceIdType.MESH
N = 64
H = N - 1
MULT = 27
OUTER = 1024
INNER = 512
SEQ = OUTER * INNER
BF = jnp.bfloat16
F32 = jnp.float32
SCALE = 1.0 / SEQ


def _circle(index, length):
    angle = 2.0 * np.pi / length * (index % length)
    return np.cos(angle), np.sin(angle)


def make_tables():
    pi = np.pi
    rows = np.arange(N)[:, None]
    lane = np.arange(128)[None, :]
    q = np.arange(16)[:, None]
    ro, x8 = q // 8, q % 8
    col = np.arange(1024)[None, :]
    a1 = 2 * pi / 128 * (rows * lane % 128)
    b1 = 2 * pi / 1024 * (x8 * col % 1024) + ro * pi / 2
    x = lane // 16 * 8 + lane % 8
    a2 = 2 * pi / 64 * (rows * x % 64)
    y = col // 16 * 8 + col % 8
    ri = col // 8 % 2
    b2 = 2 * pi / 512 * (x8 * y % 512) + (ro - ri) * pi / 2
    hh, u, c4, r4 = col // 512, col // 8 % 64, col // 2 % 4, col % 2
    c = 8 * u + 4 * hh + c4
    a4 = [2 * pi / 64 * (rows * c[:, h * 512 : h * 512 + 128] % 64) for h in range(2)]
    b4 = 2 * pi / 1024 * (q * c % 1024) + r4 * pi / 2
    half = 2 * pi / 1024 * y
    lo = (ri == 0) * np.ones((16, 1))
    hi = (ri == 1) * np.ones((16, 1))
    b2hi = b2 + ri * (pi / 2 + half)
    a3 = a2 + pi / 64 * rows
    up = col >= 512
    b3 = b2 + up * (pi / 1024 * 2 * x8 + pi)
    b3 = b3 - up * ro * pi / 2 + 0.0
    w3 = 2.0 * np.where(up, ro == 1, ro == 0)
    f = lambda m, w=1.0: np.stack([np.cos(m) * w, np.sin(m) * w])
    blocks = np.stack([f(a1), f(a2), f(a3), f(a4[0]), f(a4[1])])
    inner = np.stack(
        [f(b1), f(b2), f(b2, lo), f(b2hi, hi), f(b3, w3), f(b4, 2.0)]
    )
    return blocks.astype(np.float32), inner.astype(np.float32)


def peer(me, k):
    k = lax.rem(k * MULT, N)
    return (
        lax.rem(me // 16 + k // 16, 4) * 16
        + lax.rem(me // 4 + k // 4, 4) * 4
        + lax.rem(me // 2 + k // 2, 2) * 2
        + lax.rem(me + k, 2)
    )


def near(me, u):
    def gap(i, j):
        d = lax.rem(j - i + 4, 4)
        return jnp.minimum(d, 4 - d)

    def closer(i, j):
        return jnp.minimum(jnp.maximum(gap(3 - i, j) - gap(i, j), 0), 1)

    x = closer(me // 16, u // 16)
    z = closer(lax.rem(me // 4, 4), lax.rem(u // 4, 4))
    y = 1 - lax.rem(me // 2 + u // 2, 2)
    return x + z + y >= 2


def dot(x, y):
    return jnp.dot(x, y, preferred_element_type=F32)


def loop(n, body, start=0):
    def step(i, carry):
        body(i)
        return carry

    lax.fori_loop(start, n, step, 0)


def kernel(
    sig_h, filt_h, blk_h, inn_h, out_h,
    x1, fv, yd, ym, yq, x2, x4, y2, y3, y4,
    t1, t2, t2s, t3s, t4, wb, fw, nyq, xb, tr, acc, prod, part, blk, inn,
    ss, rs, ls,
):
    me = lax.axis_index("seq")
    ch = lax.axis_index("chan")
    bar = pltpu.get_barrier_semaphore()

    def hello(k):
        pl.semaphore_signal(bar, inc=1, device_id=(peer(me, k), ch), device_id_type=MESH)

    blk_in = pltpu.make_async_copy(blk_h, blk, ls.at[2])
    inn_in = pltpu.make_async_copy(inn_h, inn, ls.at[3])
    blk_in.start()
    inn_in.start()
    fv_in = pltpu.make_async_copy(filt_h, fv, ls.at[1])
    fv_in.start()
    loop(N, hello, 1)
    pl.semaphore_wait(bar, H)

    def remote(src, dst, s, r, p):
        return pltpu.make_async_remote_copy(
            src, dst, ss.at[s], rs.at[r], device_id=(p, ch), device_id_type=MESH
        )

    def wait_recv(r, ref):
        remote(ref, ref, 0, r, me).wait_recv()

    def wait_send(s, ref):
        remote(ref, ref, s, 0, me).wait_send()

    def copy(src, dst, s):
        return pltpu.make_async_copy(src, dst, ls.at[s])

    def send1(k):
        p = peer(me, k)
        remote(sig_h.at[:, p], x1.at[me], 0, 0, p).start()

    loop(N, send1, 1)
    own1 = copy(sig_h.at[:, me], x1.at[me], 0)
    own1.start()

    special = 1 - jnp.minimum(me, 1)
    row = lax.broadcasted_iota(jnp.int32, (16, 128), 0)
    lanes = lax.broadcasted_iota(jnp.int32, (16, 128), 1)

    def factors(i, p):
        return blk[i, 0, pl.ds(p, 1), :], blk[i, 1, pl.ds(p, 1), :]

    def tables(k):
        p = peer(me, k)
        a1 = factors(0, p)
        a2 = factors(1, p)
        a3 = factors(1 + special, p)
        a4 = (factors(3, p), factors(4, p))
        fwd = 1 + special * (1 + p // 32)
        inv = 1 + special * 3
        for j in range(8):
            cols = slice(j * 128, (j + 1) * 128)
            v = a1[0] * inn[0, 0, :, cols] - a1[1] * inn[0, 1, :, cols]
            alt = (1 - 2 * (lanes % 2)).astype(F32)
            v = jnp.where((row == 8) & (p == 0), alt, v)
            t1[k, :, cols] = v.astype(BF)
            v = a2[0] * inn[1, 0, :, cols] - a2[1] * inn[1, 1, :, cols]
            t2[k, :, cols] = v.astype(BF)
            v = a2[0] * inn[fwd, 0, :, cols] - a2[1] * inn[fwd, 1, :, cols]
            real = lanes // 8 % 2 == 0
            v = jnp.where((row == 8) & (p == 0) & (me == 0), jnp.where(real, alt, 0.0), v)
            t2s[k, :, cols] = v.astype(BF)
            a = a2 if j < 4 else a3
            v = a[0] * inn[inv, 0, :, cols] - a[1] * inn[inv, 1, :, cols]
            if j == 0:
                d0 = jnp.where(row < 8, jnp.where(lanes == 0, 1.0, (2 * (row % 2) - 1).astype(F32)), 0.0)
                v = jnp.where(((lanes == 0) | (lanes == 8)) & (me == 0), d0, v)
            t3s[k, :, cols] = v.astype(BF)
            a = a4[j // 4]
            v = a[0] * inn[5, 0, :, cols] - a[1] * inn[5, 1, :, cols]
            if j == 0:
                v = jnp.where(lanes == 0, 1.0, v)
                v = jnp.where(lanes == 1, (1 - 2 * (row % 2)).astype(F32), v)
            t4[k, :, cols] = v.astype(BF)

    blk_in.wait()
    inn_in.wait()
    loop(N, tables)

    def spread(u):
        r8 = lax.broadcasted_iota(jnp.int32, (8, 128), 0)
        l8 = lax.broadcasted_iota(jnp.int32, (8, 128), 1)
        turn = ((u * 8 + r8) * (me * 8 + l8 % 8)).astype(F32) * (2.0 * math.pi / SEQ)
        w = jnp.cos(turn - (l8 // 8).astype(F32) * (math.pi / 2))
        for j in range(16):
            wb[u, j] = jnp.broadcast_to(w[:, j : j + 1], (8, 128))

    loop(N, spread)

    fv_in.wait()
    sign = jnp.where(lax.broadcasted_iota(jnp.int32, (16, 128), 0) < 8, 1.0, -1.0)

    def direct(u):
        tr[0:128, :] = fv[:, :, u].astype(F32).reshape(128, 128)
        for c in range(8):
            yd[u, c] = tr[pl.ds(c, 16, stride=8), :].astype(BF)

    def mirrored(u):
        for p in range(2):
            for d in range(8):
                r = 128 + p * 64 + (7 - d) * 8
                tr[r : r + 8, :] = fv[p, d, 127 - u].astype(F32)
                tr[r + 128 : r + 136, :] = fv[p, d, 128 - u].astype(F32)
        ym[u, 0] = (tr[pl.ds(256, 16, stride=8), :] * sign).astype(BF)
        for c in range(1, 8):
            ym[u, c] = (tr[pl.ds(136 - c, 16, stride=8), :] * sign).astype(BF)

    def send_d(u, h):
        remote(
            yd.at[u, pl.ds(4 * h, 4)], fw.at[pl.ds(4 * h, 4), me], 1 + h, 1 + 10 * h, u
        ).start()

    def send_m(u, h):
        remote(
            ym.at[u, pl.ds(4 * h, 4)], fw.at[pl.ds(4 * h, 4), H - me], 1 + h, 1 + 10 * h, u
        ).start()

    direct(0)

    @pl.when(me >= 32)
    def _():
        tr[0:128, :] = fv[:, :, N].astype(F32).reshape(128, 128)
        yq[...] = yd[0, 0]
        yd[0, 0] = tr[pl.ds(0, 16, stride=8), :].astype(BF)

    @pl.when(me == 32)
    def _():
        remote(yq, nyq, 8, 2, 0).start()

    @pl.when(me > 0)
    def _():
        send_d(0, 0)

    def prepare(k):
        u = peer(me, k)

        @pl.when((u > 0) & near(me, u))
        def _():
            direct(u)
            mirrored(u)

            @pl.when(k > 0)
            def _():
                send_d(u, 0)
                send_m(u, 0)
                send_d(u, 1)
                send_m(u, 1)

    loop(N, prepare)

    def send_later(k):
        u = peer(me, k)

        @pl.when((u > 0) & near(me, u))
        def _():
            send_d(u, 1)
            send_m(u, 1)

    wait_recv(0, x1.at[pl.ds(0, H)])
    own1.wait()

    def relay1(i):
        v = x1[pl.ds(i * 8, 8)].astype(F32).reshape(1024, 128)
        tr[...] = v
        for b in range(8):
            xb[pl.ds(pl.multiple_of(i * 128, 128), 128), b * 128 : (b + 1) * 128] = tr[
                pl.ds(b, 128, stride=8), :
            ].astype(BF)

    loop(8, relay1)

    for j in range(4):
        cols = slice(j * 256, (j + 1) * 256)
        part[:, cols] = dot(t1[...].reshape(1024, 1024), xb[:, cols])

    def stage1(g):

        def send2(i):
            k = g * 16 + i
            p = peer(me, k)

            @pl.when((k > 0) & (i >= 0))
            def _():
                remote(y2.at[k, pl.ds(0, 4)], x2.at[pl.ds(0, 4), me], 3, 3, p).start()

        def twist(i):
            k = g * 16 + i
            u = peer(me, k)
            r0 = pl.multiple_of(k * 16, 16)
            base = 0
            for b in range(8):
                re = part[pl.ds(r0, 8), b * 128 : (b + 1) * 128]
                im = part[pl.ds(r0 + 8, 8), b * 128 : (b + 1) * 128]
                wc = wb[u, b]
                ws = wb[u, 8 + b]
                tr[pl.ds(base + b, 8, stride=16), :] = re * wc + im * ws
                tr[pl.ds(base + 8 + b, 8, stride=16), :] = im * wc - re * ws
            y2[k] = tr[0:128, :].reshape(8, 16, 128).astype(BF)
            send2(i - 1)

        loop(16, twist)
        send2(15)

    loop(4, stage1)

    for j in range(8):
        x2[j, me] = y2[0, j]

    def send2b(k):
        p = peer(me, k)
        remote(y2.at[k, pl.ds(4, 4)], x2.at[pl.ds(4, 4), me], 4, 4, p).start()

    loop(N, send2b, 1)

    @pl.when(me > 0)
    def _():
        send_d(0, 1)

    for c in range(8):
        fw[c, me] = yd[me, c]

    @pl.when(me > 0)
    def _():
        for c in range(8):
            fw[c, H - me] = ym[me, c]

    @pl.when(me == 0)
    def _():
        wait_recv(2, nyq)

    for h in range(2):
        wait_recv(3 + h, x2.at[pl.ds(4 * h, 4), pl.ds(0, H)])

        @pl.when(me == 0)
        def _():
            wait_recv(1 + 10 * h, fw.at[pl.ds(4 * h, 4), pl.ds(0, N - 1)])

        @pl.when(me > 0)
        def _():
            wait_recv(1 + 10 * h, fw.at[pl.ds(4 * h, 4), pl.ds(0, N - 2)])

        cols = [x2[4 * h + j].reshape(1024, 128) for j in range(4)]
        for j in range(4):
            xb[:, j * 128 : (j + 1) * 128] = cols[j]

        def inner(first, ref, at):
            tab = t2[...].reshape(1024, 1024)
            if h == 0:
                part[:, at : at + 128] = dot(first[...].reshape(1024, 1024), ref[:, 0:128])
                part[:, at + 128 : at + 256] = dot(tab, ref[:, 128:256])
            else:
                part[:, at : at + 256] = dot(tab, ref[:, 0:256])
            part[:, at + 256 : at + 512] = dot(tab, ref[:, 256:512])

        inner(t2s, xb, 0)

        def stage2(g):
            def multiply(i):
                v = peer(me, g * 16 + i)
                r0 = pl.multiple_of(g * 256 + i * 16, 16)
                for j in range(4):
                    sr = part[pl.ds(r0, 8), j * 128 : (j + 1) * 128]
                    si = part[pl.ds(r0 + 8, 8), j * 128 : (j + 1) * 128]
                    f = fw[4 * h + j, v].astype(F32)
                    fre = f[0:8]
                    fim = f[8:16]
                    pr = sr * fre - si * fim
                    pi = -(sr * fim + si * fre)
                    prod[pl.ds(pl.multiple_of(v * 16, 16), 16), j * 128 : (j + 1) * 128] = (
                        jnp.concatenate([pr, pi], axis=0).astype(BF)
                    )

            loop(16, multiply)
            if h == 0:

                @pl.when((me == 0) & (g == 0))
                def _():
                    sr = part[0:8, 0:128]
                    si = part[8:16, 0:128]
                    f = fw[0, 0].astype(F32)
                    fre = f[0:8]
                    fim = f[8:16]
                    rows = lax.broadcasted_iota(jnp.int32, (8, 128), 0)
                    pr = sr * fre - si * fim
                    pi = -(sr * fim + si * fre)
                    pr = jnp.where(rows == 0, sr * fre, pr)
                    pi = jnp.where(rows == 0, -(si * nyq[...].astype(F32)[0:8]), pi)
                    prod[0:16, 0:128] = jnp.concatenate([pr, pi], axis=0).astype(BF)

        loop(4, stage2)

        inner(t3s, prod, 512)

        def stage3(g):
            def send3(i):
                k = g * 16 + i
                p = peer(me, k)

                @pl.when((k > 0) & (i >= 0))
                def _():
                    remote(
                        y3.at[k, pl.ds(4 * h, 4)], x4.at[me, pl.ds(4 * h, 4)], 5 + h, 5 + h, p
                    ).start()

            def untwist(i):
                k = g * 16 + i
                t = peer(me, k)
                r0 = pl.multiple_of(k * 16, 16)
                for j in range(4):
                    re = part[pl.ds(r0, 8), 512 + j * 128 : 640 + j * 128]
                    im = part[pl.ds(r0 + 8, 8), 512 + j * 128 : 640 + j * 128]
                    wc = wb[t, 4 * h + j]
                    ws = wb[t, 8 + 4 * h + j]
                    y3[k, 4 * h + j] = jnp.concatenate(
                        [re * wc + im * ws, re * ws - im * wc], axis=0
                    ).astype(BF)
                send3(i - 1)

            loop(16, untwist)
            send3(15)

        loop(4, stage3)
        for j in range(4):
            x4[me, 4 * h + j] = y3[0, 4 * h + j]

    for h in range(2):
        wait_recv(5 + h, x4.at[pl.ds(0, H), pl.ds(4 * h, 4)])

        def relay4(i):
            v = x4[pl.ds(i * 2, 2), 4 * h : 4 * h + 4].astype(F32).reshape(128, 128)
            tr[0:128, :] = v
            for b in range(8):
                xb[pl.ds(pl.multiple_of(h * 512 + i * 16, 16), 16), b * 128 : (b + 1) * 128] = tr[
                    pl.ds(b, 16, stride=8), :
                ].astype(BF)

        loop(32, relay4)

        def stage4(g):
            rows = pl.ds(pl.multiple_of(g * 256, 256), 256)
            acc[...] = part[rows, :] + dot(
                t4[pl.ds(g * 16, 16), :, 512:1024].reshape(256, 512), xb[512:1024, :]
            )

            def send4(i):
                k = g * 16 + i
                p = peer(me, k)

                @pl.when((k > 0) & (i >= 0))
                def _():
                    remote(y4.at[k], out_h.at[:, me], 7, 7, p).start()

            def finish(i):
                k = g * 16 + i
                r0 = pl.multiple_of(i * 16, 16)
                for b in range(8):
                    tr[pl.ds(b, 16, stride=8), :] = acc[pl.ds(r0, 16), b * 128 : (b + 1) * 128]
                y4[k] = (tr[0:128, :] * SCALE).reshape(16, 8, 128).astype(BF)
                send4(i - 1)

            loop(16, finish)
            send4(15)

        if h == 0:
            for j in range(4):
                cols = slice(j * 256, (j + 1) * 256)
                part[:, cols] = dot(t4[:, :, 0:512].reshape(1024, 512), xb[0:512, cols])
        else:
            loop(4, stage4)

    own4 = copy(y4.at[0], out_h.at[:, me], 10)
    own4.start()
    wait_send(0, sig_h.at[:, pl.ds(0, H)])
    near0 = near(me, 0)

    def drained(n):
        for h in range(2):
            wait_send(1 + h, yd.at[pl.ds(0, n), pl.ds(4 * h, 4)])

    @pl.when(me == 0)
    def _():
        drained(62)

    @pl.when((me > 0) & near0)
    def _():
        drained(61)

    @pl.when((me > 0) & jnp.logical_not(near0))
    def _():
        drained(63)

    @pl.when(me == 32)
    def _():
        wait_send(8, yq)

    for h in range(2):
        wait_send(3 + h, y2.at[pl.ds(0, H), pl.ds(4 * h, 4)])
        wait_send(5 + h, y3.at[pl.ds(0, H), pl.ds(4 * h, 4)])
    wait_send(7, y4.at[pl.ds(0, H)])
    wait_recv(7, out_h.at[:, pl.ds(0, H)])
    own4.wait()


def local(signal, gate_values, skip_gain, filter_spectrum):
    blocks, inner = make_tables()
    any_ = pl.BlockSpec(memory_space=pl.ANY)
    hbm = pl.BlockSpec(memory_space=pltpu.HBM)
    V = pltpu.VMEM
    dma = pltpu.SemaphoreType.DMA
    out = pl.pallas_call(
        kernel,
        out_shape=jax.ShapeDtypeStruct((16, 64, 8, 128), BF),
        in_specs=[hbm, hbm, hbm, hbm],
        out_specs=any_,
        scratch_shapes=[
            V((64, 16, 8, 128), BF),
            V((2, 8, 128, 8, 128), BF),
            V((64, 8, 16, 128), BF),
            V((64, 8, 16, 128), BF),
            V((16, 128), BF),
            V((8, 64, 16, 128), BF),
            V((64, 8, 16, 128), BF),
            V((64, 8, 16, 128), BF),
            V((64, 8, 16, 128), BF),
            V((64, 16, 8, 128), BF),
            V((64, 16, 1024), BF),
            V((64, 16, 1024), BF),
            V((64, 16, 1024), BF),
            V((64, 16, 1024), BF),
            V((64, 16, 1024), BF),
            V((64, 16, 8, 128), F32),
            V((8, 64, 16, 128), BF),
            V((16, 128), BF),
            V((1024, 1024), BF),
            V((1024, 128), F32),
            V((256, 1024), F32),
            V((1024, 512), BF),
            V((1024, 1024), F32),
            V((5, 2, N, 128), F32),
            V((6, 2, 16, 1024), F32),
            dma((9,)),
            dma((12,)),
            dma((12,)),
        ],
        compiler_params=pltpu.CompilerParams(
            collective_id=0, has_side_effects=True, vmem_limit_bytes=58 << 20
        ),
    )(
        signal.reshape(16, 64, 8, 128),
        filter_spectrum.reshape(2, 8, 128, 8, 128),
        jnp.asarray(blocks),
        jnp.asarray(inner),
    )
    grid = (16, 64, 8, 128)
    skipped = skip_gain * signal.reshape(grid).astype(F32)
    result = gate_values.reshape(grid).astype(F32) * (out.astype(F32) + skipped)
    return result.astype(BF).reshape(8192, 128)


def solution(mesh):
    return jax.shard_map(
        local,
        mesh=mesh,
        in_specs=(P("seq", "chan"), P("seq", "chan"), P("chan"), P(None, "seq", None, "chan")),
        out_specs=P("seq", "chan"),
        check_vma=False,
    )
```

time: 158 us -> 151 us (0.956)
  the two profiles are of different devices: /device:TPU:1 before, /device:TPU:24 now
where the time goes in v2:
time: 151 us
  Pallas kernels  147 us (97%)
  other arithmetic  3.93 us (3%)
    pallas_call x1, Pallas kernels, local(): pl.pallas_call(kernel, out_shape=jax.ShapeDtypeStruct((16, 64, 8, 128), B...  147 us
    convert_element_type x1, other arithmetic, local(): return result.astype(BF).reshape(8192, 128)  3.93 us

profile of v2, /device:TPU:24, one launch (start us, length us, event | category | flops | bytes accessed | tf_op | source)
XLA Modules:
  0.0 150.8 jit_solution(14083540663620326160)
XLA Ops:
  0.0 0.0 copy-start
  0.0 0.0 copy-start.1
  0.0 0.0 copy-start.2
  0.0 146.8 %shard_map.64 = bf16[16,64,8,128]{3,2,1,0:T(8,128)(2,1)} custom-call(bf16[16,64,8,128]{3,2,1,0:T(8,128)(2,1)} %bitcast.5, bf16[2,8,128,8,128]{4,3,2,1,0:T(8,128)(2,1)} %bitcast.7, f32[5,2,64,128]{3,2,1,0:T(8,128)} %constant.4.clone.blk_h, f32[6,2,16,1024]{3,2,1,0:T(8,128)} %constant.5.clone.inn_h), custom_call_target="tpu_custom_call" | custom-call | tf_op jit(solution)/shard_map/pallas_call | solution.py:517
  146.8 0.0 copy-done
  146.8 0.0 copy-done.1
  146.9 0.0 copy-done.2
  146.9 3.9 %fusion = bf16[16,64,8,128]{3,2,1,0:T(8,128)(2,1)} fusion(bf16[16,64,8,128]{3,2,1,0:T(8,128)(2,1)S(1)} %bitcast.8, bf16[16,64,8,128]{3,2,1,0:T(8,128)(2,1)S(1)} %bitcast.6, bf16[16,64,8,128]{3,2,1,0:T(8,128)(2,1)} %shard_map.64, f32[128]{0:T(128)S(1)} %copy-done.2), kind=kLoop, calls=%fused_computation.1 | loop fusion | flops 7340032 | bytes 8389120 | tf_op jit(solution)/shard_map/convert_element_type | solution.py:564
Async XLA Ops:
  0.0 146.8 %copy-start = (bf16[8192,128]{1,0:T(8,128)(2,1)S(1)}, bf16[8192,128]{1,0:T(8,128)(2,1)}, u32[]{:S(2)}) copy-start(bf16[8192,128]{1,0:T(8,128)(2,1)} %param.6) | copy-start | bytes 6291460
  0.0 146.8 %copy-start.1 = (bf16[8192,128]{1,0:T(8,128)(2,1)S(1)}, bf16[8192,128]{1,0:T(8,128)(2,1)}, u32[]{:S(2)}) copy-start(bf16[8192,128]{1,0:T(8,128)(2,1)} %param.7) | copy-start | bytes 6291460
  0.0 146.9 %copy-start.2 = (f32[128]{0:T(128)S(1)}, f32[128]{0:T(128)}, u32[]{:S(2)}) copy-start(f32[128]{0:T(128)} %param.8) | copy-start | bytes 1540

commit v3 on v2

--- a/solution.py
+++ b/solution.py
@@ -11,7 +11,7 @@
 MESH = pl.DeviceIdType.MESH
 N = 64
 H = N - 1
-MULT = 27
+MULT = 37
 OUTER = 1024
 INNER = 512
 SEQ = OUTER * INNER
@@ -184,16 +184,6 @@
     inn_in.wait()
     loop(N, tables)
 
-    def spread(u):
-        r8 = lax.broadcasted_iota(jnp.int32, (8, 128), 0)
-        l8 = lax.broadcasted_iota(jnp.int32, (8, 128), 1)
-        turn = ((u * 8 + r8) * (me * 8 + l8 % 8)).astype(F32) * (2.0 * math.pi / SEQ)
-        w = jnp.cos(turn - (l8 // 8).astype(F32) * (math.pi / 2))
-        for j in range(16):
-            wb[u, j] = jnp.broadcast_to(w[:, j : j + 1], (8, 128))
-
-    loop(N, spread)
-
     fv_in.wait()
     sign = jnp.where(lax.broadcasted_iota(jnp.int32, (16, 128), 0) < 8, 1.0, -1.0)
 
@@ -255,13 +245,15 @@
 
     loop(N, prepare)
 
-    def send_later(k):
-        u = peer(me, k)
-
-        @pl.when((u > 0) & near(me, u))
-        def _():
-            send_d(u, 1)
-            send_m(u, 1)
+    def spread(u):
+        r8 = lax.broadcasted_iota(jnp.int32, (8, 128), 0)
+        l8 = lax.broadcasted_iota(jnp.int32, (8, 128), 1)
+        turn = ((u * 8 + r8) * (me * 8 + l8 % 8)).astype(F32) * (2.0 * math.pi / SEQ)
+        w = jnp.cos(turn - (l8 // 8).astype(F32) * (math.pi / 2))
+        for j in range(16):
+            wb[u, j] = jnp.broadcast_to(w[:, j : j + 1], (8, 128))
+
+    loop(N, spread)
 
     wait_recv(0, x1.at[pl.ds(0, H)])
     own1.wait()

time: 151 us -> 145 us (0.960)
  the two profiles are of different devices: /device:TPU:24 before, /device:TPU:1 now
where the time goes in v3:
time: 145 us
  Pallas kernels  141 us (97%)
  other arithmetic  3.93 us (3%)
    pallas_call x1, Pallas kernels, local(): pl.pallas_call(kernel, out_shape=jax.ShapeDtypeStruct((16, 64, 8, 128), B...  141 us
    convert_element_type x1, other arithmetic, local(): return result.astype(BF).reshape(8192, 128)  3.93 us

profile of v3, /device:TPU:1, one launch (start us, length us, event | category | flops | bytes accessed | tf_op | source)
XLA Modules:
  0.0 144.9 jit_solution(13917307264999191251)
XLA Ops:
  0.0 0.0 copy-start
  0.0 0.0 copy-start.1
  0.0 0.0 copy-start.2
  0.0 140.9 %shard_map.64 = bf16[16,64,8,128]{3,2,1,0:T(8,128)(2,1)} custom-call(bf16[16,64,8,128]{3,2,1,0:T(8,128)(2,1)} %bitcast.5, bf16[2,8,128,8,128]{4,3,2,1,0:T(8,128)(2,1)} %bitcast.7, f32[5,2,64,128]{3,2,1,0:T(8,128)} %constant.4.clone.blk_h, f32[6,2,16,1024]{3,2,1,0:T(8,128)} %constant.5.clone.inn_h), custom_call_target="tpu_custom_call" | custom-call | tf_op jit(solution)/shard_map/pallas_call | solution.py:509
  140.9 0.0 copy-done
  140.9 0.0 copy-done.1
  140.9 0.0 copy-done.2
  141.0 3.9 %fusion = bf16[16,64,8,128]{3,2,1,0:T(8,128)(2,1)} fusion(bf16[16,64,8,128]{3,2,1,0:T(8,128)(2,1)S(1)} %bitcast.8, bf16[16,64,8,128]{3,2,1,0:T(8,128)(2,1)S(1)} %bitcast.6, bf16[16,64,8,128]{3,2,1,0:T(8,128)(2,1)} %shard_map.64, f32[128]{0:T(128)S(1)} %copy-done.2), kind=kLoop, calls=%fused_computation.1 | loop fusion | flops 7340032 | bytes 8389120 | tf_op jit(solution)/shard_map/convert_element_type | solution.py:556
Async XLA Ops:
  0.0 140.9 %copy-start = (bf16[8192,128]{1,0:T(8,128)(2,1)S(1)}, bf16[8192,128]{1,0:T(8,128)(2,1)}, u32[]{:S(2)}) copy-start(bf16[8192,128]{1,0:T(8,128)(2,1)} %param.6) | copy-start | bytes 6291460
  0.0 140.9 %copy-start.1 = (bf16[8192,128]{1,0:T(8,128)(2,1)S(1)}, bf16[8192,128]{1,0:T(8,128)(2,1)}, u32[]{:S(2)}) copy-start(bf16[8192,128]{1,0:T(8,128)(2,1)} %param.7) | copy-start | bytes 6291460
  0.0 140.9 %copy-start.2 = (f32[128]{0:T(128)S(1)}, f32[128]{0:T(128)}, u32[]{:S(2)}) copy-start(f32[128]{0:T(128)} %param.8) | copy-start | bytes 1540

commit v4 on v3

--- a/solution.py
+++ b/solution.py
@@ -260,7 +260,7 @@
 
     def relay1(i):
         v = x1[pl.ds(i * 8, 8)].astype(F32).reshape(1024, 128)
-        tr[...] = v
+        tr[0:1024, :] = v
         for b in range(8):
             xb[pl.ds(pl.multiple_of(i * 128, 128), 128), b * 128 : (b + 1) * 128] = tr[
                 pl.ds(b, 128, stride=8), :
@@ -531,7 +531,7 @@
             V((8, 64, 16, 128), BF),
             V((16, 128), BF),
             V((1024, 1024), BF),
-            V((1024, 128), F32),
+            V((1152, 128), F32),
             V((256, 1024), F32),
             V((1024, 512), BF),
             V((1024, 1024), F32),

time: 145 us -> 145 us (level)
  no operation moved by 1% of the time
where the time goes in v4:
time: 145 us
  Pallas kernels  141 us (97%)
  other arithmetic  3.93 us (3%)
    pallas_call x1, Pallas kernels, local(): pl.pallas_call(kernel, out_shape=jax.ShapeDtypeStruct((16, 64, 8, 128), B...  141 us
    convert_element_type x1, other arithmetic, local(): return result.astype(BF).reshape(8192, 128)  3.93 us

profile of v4, /device:TPU:1, one launch (start us, length us, event | category | flops | bytes accessed | tf_op | source)
XLA Modules:
  0.0 144.9 jit_solution(4301540571252669407)
XLA Ops:
  0.0 0.0 copy-start
  0.0 0.0 copy-start.1
  0.0 0.0 copy-start.2
  0.0 140.9 %shard_map.64 = bf16[16,64,8,128]{3,2,1,0:T(8,128)(2,1)} custom-call(bf16[16,64,8,128]{3,2,1,0:T(8,128)(2,1)} %bitcast.5, bf16[2,8,128,8,128]{4,3,2,1,0:T(8,128)(2,1)} %bitcast.7, f32[5,2,64,128]{3,2,1,0:T(8,128)} %constant.4.clone.blk_h, f32[6,2,16,1024]{3,2,1,0:T(8,128)} %constant.5.clone.inn_h), custom_call_target="tpu_custom_call" | custom-call | tf_op jit(solution)/shard_map/pallas_call | solution.py:509
  140.9 0.0 copy-done
  140.9 0.0 copy-done.1
  140.9 0.0 copy-done.2
  141.0 3.9 %fusion = bf16[16,64,8,128]{3,2,1,0:T(8,128)(2,1)} fusion(bf16[16,64,8,128]{3,2,1,0:T(8,128)(2,1)S(1)} %bitcast.8, bf16[16,64,8,128]{3,2,1,0:T(8,128)(2,1)S(1)} %bitcast.6, bf16[16,64,8,128]{3,2,1,0:T(8,128)(2,1)} %shard_map.64, f32[128]{0:T(128)S(1)} %copy-done.2), kind=kLoop, calls=%fused_computation.1 | loop fusion | flops 7340032 | bytes 8389120 | tf_op jit(solution)/shard_map/convert_element_type | solution.py:556
Async XLA Ops:
  0.0 140.9 %copy-start = (bf16[8192,128]{1,0:T(8,128)(2,1)S(1)}, bf16[8192,128]{1,0:T(8,128)(2,1)}, u32[]{:S(2)}) copy-start(bf16[8192,128]{1,0:T(8,128)(2,1)} %param.6) | copy-start | bytes 6291460
  0.0 140.9 %copy-start.1 = (bf16[8192,128]{1,0:T(8,128)(2,1)S(1)}, bf16[8192,128]{1,0:T(8,128)(2,1)}, u32[]{:S(2)}) copy-start(bf16[8192,128]{1,0:T(8,128)(2,1)} %param.7) | copy-start | bytes 6291460
  0.0 140.9 %copy-start.2 = (f32[128]{0:T(128)S(1)}, f32[128]{0:T(128)}, u32[]{:S(2)}) copy-start(f32[128]{0:T(128)} %param.8) | copy-start | bytes 1540

commit v5 on v4

--- a/solution.py
+++ b/solution.py
@@ -11,7 +11,7 @@
 MESH = pl.DeviceIdType.MESH
 N = 64
 H = N - 1
-MULT = 37
+MULT = 45
 OUTER = 1024
 INNER = 512
 SEQ = OUTER * INNER

time: 145 us -> 145 us (level)
  no operation moved by 1% of the time
where the time goes in v5:
time: 145 us; the launch traced here: 144 us
  Pallas kernels  140 us (97%)
  other arithmetic  3.93 us (3%)
    pallas_call x1, Pallas kernels, local(): pl.pallas_call(kernel, out_shape=jax.ShapeDtypeStruct((16, 64, 8, 128), B...  140 us
    convert_element_type x1, other arithmetic, local(): return result.astype(BF).reshape(8192, 128)  3.93 us

profile of v5, /device:TPU:1, one launch (start us, length us, event | category | flops | bytes accessed | tf_op | source)
XLA Modules:
  0.0 144.3 jit_solution(14117702249059724815)
XLA Ops:
  0.0 0.0 copy-start
  0.0 0.0 copy-start.1
  0.0 0.0 copy-start.2
  0.0 140.3 %shard_map.64 = bf16[16,64,8,128]{3,2,1,0:T(8,128)(2,1)} custom-call(bf16[16,64,8,128]{3,2,1,0:T(8,128)(2,1)} %bitcast.5, bf16[2,8,128,8,128]{4,3,2,1,0:T(8,128)(2,1)} %bitcast.7, f32[5,2,64,128]{3,2,1,0:T(8,128)} %constant.4.clone.blk_h, f32[6,2,16,1024]{3,2,1,0:T(8,128)} %constant.5.clone.inn_h), custom_call_target="tpu_custom_call" | custom-call | tf_op jit(solution)/shard_map/pallas_call | solution.py:509
  140.3 0.0 copy-done
  140.3 0.0 copy-done.1
  140.3 0.0 copy-done.2
  140.3 3.9 %fusion = bf16[16,64,8,128]{3,2,1,0:T(8,128)(2,1)} fusion(bf16[16,64,8,128]{3,2,1,0:T(8,128)(2,1)S(1)} %bitcast.8, bf16[16,64,8,128]{3,2,1,0:T(8,128)(2,1)S(1)} %bitcast.6, bf16[16,64,8,128]{3,2,1,0:T(8,128)(2,1)} %shard_map.64, f32[128]{0:T(128)S(1)} %copy-done.2), kind=kLoop, calls=%fused_computation.1 | loop fusion | flops 7340032 | bytes 8389120 | tf_op jit(solution)/shard_map/convert_element_type | solution.py:556
Async XLA Ops:
  0.0 140.3 %copy-start = (bf16[8192,128]{1,0:T(8,128)(2,1)S(1)}, bf16[8192,128]{1,0:T(8,128)(2,1)}, u32[]{:S(2)}) copy-start(bf16[8192,128]{1,0:T(8,128)(2,1)} %param.6) | copy-start | bytes 6291460
  0.0 140.3 %copy-start.1 = (bf16[8192,128]{1,0:T(8,128)(2,1)S(1)}, bf16[8192,128]{1,0:T(8,128)(2,1)}, u32[]{:S(2)}) copy-start(bf16[8192,128]{1,0:T(8,128)(2,1)} %param.7) | copy-start | bytes 6291460
  0.0 140.3 %copy-start.2 = (f32[128]{0:T(128)S(1)}, f32[128]{0:T(128)}, u32[]{:S(2)}) copy-start(f32[128]{0:T(128)} %param.8) | copy-start | bytes 1540
